TPU v7x, 32 devices: a whole 2x2x4 slice. The times are simulated.
32 devices in a mesh: level: 2 (over x), row: 4 (over y, core), col: 4 (over z).
Axes of the slice: x: 2, y: 2, z: 4, core: 2. Of those that a mesh axis runs over, the one named last changes fastest.
Arguments:
- initial: float32 [3, 512, 4096], P(None, 'row', 'col'), may hold values from -0.75 to 0.75
Outputs:
- levels_out: float32 [2, 3, 512, 4096], P('level', None, 'row', 'col')
All inputs are finite; a program needn't handle non-finite values.
Results may differ from a plain program's by a relative error of at most 0.00002.
Values sent between devices are 32-bit elements; how exact they have to be, the bound alone decides.
A program may use at most 64 MiB of HBM per device.

v0:
```python
import functools

import jax
import jax.numpy as jnp
from jax import lax
from jax.experimental import pallas as pl
from jax.experimental.pallas import tpu as pltpu
from jax.sharding import PartitionSpec as P

STEPS = 8
time_step = 0.1
gravity = 1.0
rotation = 0.2

MESH = pl.DeviceIdType.MESH
LANES = 128
SUBS = 8
DEPTH = STEPS + 1
PACK = 16
TOP = 16

VEL = 0.5 * time_step
ELEV = VEL * VEL * gravity
TURN = time_step * rotation


def exchange(
    tile, rows, nine, cols, diag, top, bottom, edges, nine_out, pack, load_sem, send_sem, recv_sem
):
    fields, height, width = tile.shape
    n_row, n_col = lax.axis_size("row"), lax.axis_size("col")
    r, c = lax.axis_index("row"), lax.axis_index("col")
    up, down = lax.rem(r + n_row - 1, n_row), lax.rem(r + 1, n_row)
    left, right = lax.rem(c + n_col - 1, n_col), lax.rem(c + 1, n_col)
    loads = [
        pltpu.make_async_copy(tile.at[:, :, pl.ds(0, LANES)], edges.at[0], load_sem.at[0]),
        pltpu.make_async_copy(tile.at[:, :, pl.ds(width - LANES, LANES)], edges.at[1], load_sem.at[1]),
        pltpu.make_async_copy(tile.at[:, pl.ds(0, 16), :], top, load_sem.at[2]),
        pltpu.make_async_copy(tile.at[:, pl.ds(height - 16, 16), :], bottom, load_sem.at[3]),
    ]
    for load in loads:
        load.start()
    barrier = pltpu.get_barrier_semaphore()
    around = [(up, c), (down, c), (r, left), (r, right), (up, left), (up, right), (down, left), (down, right)]
    for to_r, to_c in around:
        pl.semaphore_signal(barrier, inc=1, device_id={"row": to_r, "col": to_c}, device_id_type=MESH)
    for load in loads:
        load.wait()
    tiles = width // LANES
    for f in range(fields):
        for t in range(tiles):
            nine_out[0, pl.ds(f * tiles + t, 1), :] = top[f, pl.ds(8, 1), pl.ds(t * LANES, LANES)]
            nine_out[1, pl.ds(f * tiles + t, 1), :] = bottom[f, pl.ds(7, 1), pl.ds(t * LANES, LANES)]
    lane_group = lax.broadcasted_iota(jnp.int32, (SUBS, LANES), 1) // PACK
    per = LANES // PACK
    for side in range(2):
        first = 0 if side == 0 else LANES - PACK
        for half in range(2):
            for f in range(fields):
                packed = None
                for g in range(per):
                    block = edges[side, f, pl.ds((half * per + g) * SUBS, SUBS), :]
                    amount = (g * PACK - first) % LANES
                    moved = pltpu.roll(block, amount, 1) if amount else block
                    packed = moved if packed is None else jnp.where(lane_group == g, moved, packed)
                pack[side, half, f] = packed
    pl.semaphore_wait(barrier, len(around))
    moves = [
        (top.at[:, pl.ds(0, 8), :], rows.at[1], up, c),
        (bottom.at[:, pl.ds(8, 8), :], rows.at[0], down, c),
        (pack.at[0, 0], diag.at[3], up, left),
        (pack.at[1, 0], diag.at[2], up, right),
        (pack.at[0, 1], diag.at[1], down, left),
        (pack.at[1, 1], diag.at[0], down, right),
        (pack.at[0], cols.at[1], r, left),
        (pack.at[1], cols.at[0], r, right),
        (nine_out.at[0], nine.at[1], up, c),
        (nine_out.at[1], nine.at[0], down, c),
    ]
    sends = [
        pltpu.make_async_remote_copy(
            src_ref=src,
            dst_ref=dst,
            send_sem=send_sem.at[i],
            recv_sem=recv_sem.at[i],
            device_id={"row": to_r, "col": to_c},
            device_id_type=MESH,
        )
        for i, (src, dst, to_r, to_c) in enumerate(moves)
    ]
    for send in sends:
        send.start()
    for send in sends:
        send.wait()


def call_exchange(initial):
    fields, height, width = initial.shape
    nine_rows = fields * width // LANES
    shape = functools.partial(jax.ShapeDtypeStruct, dtype=jnp.float32)
    vmem = lambda *dims: pltpu.VMEM(dims, jnp.float32)
    anywhere = pl.BlockSpec(memory_space=pl.ANY)
    return pl.pallas_call(
        exchange,
        out_shape=(
            shape((2, fields, 8, width)),
            shape((2, nine_rows, LANES)),
            shape((2, 2, fields, SUBS, LANES)),
            shape((4, fields, SUBS, LANES)),
        ),
        in_specs=[anywhere],
        out_specs=(anywhere,) * 4,
        scratch_shapes=[
            vmem(fields, 16, width),
            vmem(fields, 16, width),
            vmem(2, fields, height, LANES),
            vmem(2, nine_rows, LANES),
            vmem(2, 2, fields, SUBS, LANES),
            pltpu.SemaphoreType.DMA((4,)),
            pltpu.SemaphoreType.DMA((10,)),
            pltpu.SemaphoreType.DMA((10,)),
        ],
        compiler_params=pltpu.CompilerParams(
            collective_id=0, has_side_effects=True, vmem_limit_bytes=8 * 1024 * 1024
        ),
        name="exchange",
    )(initial)


def along_cols(x):
    return pltpu.roll(x, LANES - 1, 1) - pltpu.roll(x, 1, 1)


def full(state):
    e, u, v = state
    h = ELEV + e
    return e, u, v, h * u, h * v


def change(above, here, below):
    e0, u0, v0, hu0, _ = above
    e, u, v, _, hv = here
    e1, u1, v1, hu1, _ = below
    return (
        (hu1 - hu0) + along_cols(hv),
        u * (u1 - u0) + v * (along_cols(u) - TURN) + (e1 - e0),
        u * ((v1 - v0) + TURN) + v * along_cols(v) + along_cols(e),
    )


def row_of(ref, k):
    return tuple(ref[f, k] for f in range(3))


def put_row(ref, k, values):
    for f in range(3):
        ref[f, k] = values[f]


def from_above(state):
    return tuple(pltpu.roll(x, 1, 0) for x in state)


def from_below(state):
    return tuple(pltpu.roll(x, SUBS - 1, 0) for x in state)


def minus(state, rate):
    return tuple(a - b for a, b in zip(state, rate))


def minus_half(state, rate):
    return tuple(a - 0.5 * b for a, b in zip(state, rate))


def sweep(ref, use):
    count = ref.shape[1]
    above = full(from_above(row_of(ref, count - 1)))
    here = first = full(row_of(ref, 0))
    last = full(from_below(first[:3]))
    for k in range(count):
        below = last if k == count - 1 else full(row_of(ref, k + 1))
        use(k, here[:3], change(above, here, below))
        above, here = here, below


def predict(pred):
    sweep(pred, lambda k, state, rate: put_row(pred, k, minus(state, rate)))


def first_step(pred, base):
    def use(k, state, rate):
        put_row(pred, k, minus(state, rate))
        put_row(base, k, minus_half(state, rate))

    sweep(pred, use)


def middle_step(pred, base):
    count = pred.shape[1]
    corr = {}

    def correct(k, above, here, below):
        put_row(base, k, minus(row_of(base, k), change(above, here, below)))

    def use(k, state, rate):
        put_row(pred, k, minus(state, rate))
        corr[k] = full(minus_half(row_of(base, k), rate))
        if k >= 2:
            correct(k - 1, corr[k - 2], corr[k - 1], corr[k])

    sweep(pred, use)
    end = count - 1
    correct(end, corr[end - 1], corr[end], full(from_below(corr[0][:3])))
    correct(0, full(from_above(corr[end][:3])), corr[0], corr[1])


def last_step(pred, base):
    sweep(pred, lambda k, state, rate: put_row(pred, k, minus_half(row_of(base, k), rate)))


def strip_plan(width):
    for strips in range(width // LANES + 1, 4 * (width // LANES) + 4):
        for stride in range(-(-width // strips), LANES - 2 * DEPTH + 1):
            done = [min(width // LANES, stride * (t + 1) // LANES) for t in range(strips)]
            gaps = all(stride * t % LANES >= DEPTH for t in range(1, strips))
            if gaps and done[-1] == width // LANES and (strips - 1) * stride < width:
                return strips, stride


def window(
    tile, rows, nine, cols, diag, out, padded, result, pred, base, load_sem, halo_sem, out_sem
):
    fields, height, width = tile.shape
    tiles = width // LANES
    count = pred.shape[1]
    strips, stride = strip_plan(width)
    level = lax.axis_index("level")
    loads = []
    for j in range(tiles):
        lanes = pl.ds(j * LANES, LANES)
        loads += [
            pltpu.make_async_copy(
                tile.at[:, :, lanes], padded.at[:, j + 1, pl.ds(TOP, height), :], load_sem.at[j]
            ),
            pltpu.make_async_copy(
                rows.at[0, :, :, lanes], padded.at[:, j + 1, pl.ds(TOP - 8, 8), :], halo_sem.at[0, j]
            ),
            pltpu.make_async_copy(
                rows.at[1, :, :, lanes], padded.at[:, j + 1, pl.ds(TOP + height, 8), :], halo_sem.at[1, j]
            ),
        ]
    for load in loads:
        load.start()
    per = LANES // PACK

    def unpack(side, f, at, block, g):
        amount = ((LANES - PACK if side == 0 else 0) - g * PACK) % LANES
        moved = pltpu.roll(block, amount, 1) if amount else block
        padded[f, 0 if side == 0 else tiles + 1, pl.ds(at, SUBS), :] = moved

    for side in range(2):
        for f in range(fields):
            for half in range(2):
                block = cols[side, half, f]
                for g in range(per):
                    unpack(side, f, TOP + (half * per + g) * SUBS, block, g)
            for i in range(2):
                unpack(side, f, TOP - 16 + i * SUBS, diag[side, f], per - 2 + i)
                unpack(side, f, TOP + height + i * SUBS, diag[2 + side, f], i)
    for f in range(fields):
        for j in range(tiles):
            padded[f, j + 1, pl.ds(TOP - DEPTH, 1), :] = nine[0, pl.ds(f * tiles + j, 1), :]
            padded[f, j + 1, pl.ds(TOP + height + DEPTH - 1, 1), :] = nine[1, pl.ds(f * tiles + j, 1), :]
    for load in loads:
        load.wait()

    lane = lax.broadcasted_iota(jnp.int32, (SUBS, LANES), 1)
    into = (ELEV, VEL, VEL)

    def out_copy(j):
        return pltpu.make_async_copy(
            result.at[:, j + 1, pl.ds(TOP, height), :],
            out.at[0, :, :, pl.ds(pl.multiple_of(j * LANES, LANES), LANES)],
            out_sem.at[j],
        )

    def strip(t, carry):
        start = t * stride + LANES - DEPTH
        a = start // LANES
        offset = start - a * LANES
        from_first = lane >= offset
        for f in range(fields):
            for k in range(count):
                at = pl.ds(TOP - DEPTH + k, SUBS, stride=count)
                both = jnp.where(from_first, padded[f, a, at, :], padded[f, a + 1, at, :])
                pred[f, k] = into[f] * pltpu.roll(both, LANES - offset, 1)

        @pl.when(level == 0)
        def _():
            lax.fori_loop(0, STEPS, lambda m, x: (predict(pred), x)[1], 0)

        @pl.when(level == 1)
        def _():
            first_step(pred, base)
            lax.fori_loop(1, STEPS, lambda m, x: (middle_step(pred, base), x)[1], 0)
            last_step(pred, base)

        source = jnp.where(from_first, lane - offset, lane - offset + LANES)
        inside = (source >= DEPTH) & (source < DEPTH + stride)
        low, high = from_first & inside, jnp.logical_not(from_first) & inside
        for f in range(fields):
            for k in range(count):
                at = pl.ds(TOP - DEPTH + k, SUBS, stride=count)
                moved = pltpu.roll((1.0 / into[f]) * pred[f, k], offset, 1)
                result[f, a, at, :] = jnp.where(low, moved, result[f, a, at, :])
                result[f, a + 1, at, :] = jnp.where(high, moved, result[f, a + 1, at, :])
        done = jnp.minimum(tiles, (t + 1) * stride // LANES)
        before = jnp.minimum(tiles, t * stride // LANES)

        @pl.when(done > before)
        def _():
            out_copy(done - 1).start()

        return carry

    lax.fori_loop(0, strips, strip, 0)
    for j in range(tiles):
        out_copy(j).wait()


def call_window(initial, rows, nine, cols, diag):
    fields, height, width = initial.shape
    tiles = width // LANES
    count = -(-(height + 2 * DEPTH) // SUBS)
    padded_rows = height + 2 * TOP
    vmem = lambda *dims: pltpu.VMEM(dims, jnp.float32)
    anywhere = pl.BlockSpec(memory_space=pl.ANY)
    local = pl.BlockSpec(memory_space=pltpu.VMEM)
    return pl.pallas_call(
        window,
        out_shape=jax.ShapeDtypeStruct((1, fields, height, width), jnp.float32),
        in_specs=[anywhere, anywhere, local, local, local],
        out_specs=anywhere,
        scratch_shapes=[
            vmem(fields, tiles + 2, padded_rows, LANES),
            vmem(fields, tiles + 2, padded_rows, LANES),
            vmem(fields, count, SUBS, LANES),
            vmem(fields, count, SUBS, LANES),
            pltpu.SemaphoreType.DMA((tiles,)),
            pltpu.SemaphoreType.DMA((2, tiles)),
            pltpu.SemaphoreType.DMA((tiles,)),
        ],
        compiler_params=pltpu.CompilerParams(vmem_limit_bytes=16 * 1024 * 1024),
        name="window",
    )(initial, rows, nine, cols, diag)


def body(initial):
    return call_window(initial, *call_exchange(initial))


def solution(mesh):
    return jax.shard_map(
        body,
        mesh=mesh,
        in_specs=(P(None, "row", "col"),),
        out_specs=P("level", None, "row", "col"),
        check_vma=False,
    )
```

profile of v0, /device:TPU:7, one launch (start us, length us, event | category | flops | bytes accessed | tf_op | source)
XLA Modules:
  0.0 68.7 jit_solution(1882954994071943845)
XLA Ops:
  0.0 0.0 copy-start
  0.0 1.4 %copy-done = f32[3,128,1024]{2,1,0:T(8,128)S(1)} copy-done((f32[3,128,1024]{2,1,0:T(8,128)S(1)}, f32[3,128,1024]{2,1,0:T(8,128)}, u32[]{:S(2)}) %copy-start) | copy-done | bytes 1572888
  1.4 0.0 copy-start.1
  1.4 9.4 %exchange.1 = (f32[2,3,8,1024]{3,2,1,0:T(8,128)S(1)}, f32[2,24,128]{2,1,0:T(8,128)S(1)}, f32[2,2,3,8,128]{4,3,2,1,0:T(8,128)S(1)}, f32[4,3,8,128]{3,2,1,0:T(8,128)S(1)}) custom-call(f32[3,128,1024]{2,1,0:T(8,128)S(1)} %copy-done), custom_call_target="tpu_custom_call" | custom-call | tf_op jit(solution)/shard_map/exchange/pallas_call | solution.py:103
  10.8 0.0 copy-done.1
  10.8 57.9 %window.1 = f32[1,3,128,1024]{3,2,1,0:T(8,128)} custom-call(f32[3,128,1024]{2,1,0:T(8,128)S(1)} %copy-done.1, f32[2,3,8,1024]{3,2,1,0:T(8,128)S(1)} %get-tuple-element.9.rows, f32[2,24,128]{2,1,0:T(8,128)S(1)} %get-tuple-element.10.nine, f32[2,2,3,8,128]{4,3,2,1,0:T(8,128)S(1)} %get-tuple-element.11.cols, f32[4,3,8,128]{3,2,1,0:T(8,128)S(1)} %get-tuple-element.12.diag), custom_call_target="tpu_custom_call" | custom-call | tf_op jit(solution)/shard_map/window/pallas_call | solution.py:340
Async XLA Ops:
  0.0 1.4 %copy-start = (f32[3,128,1024]{2,1,0:T(8,128)S(1)}, f32[3,128,1024]{2,1,0:T(8,128)}, u32[]{:S(2)}) copy-start(f32[3,128,1024]{2,1,0:T(8,128)} %tile.3) | copy-start | bytes 4718596
  1.4 9.4 %copy-start.1 = (f32[3,128,1024]{2,1,0:T(8,128)S(1)}, f32[3,128,1024]{2,1,0:T(8,128)}, u32[]{:S(2)}) copy-start(f32[3,128,1024]{2,1,0:T(8,128)} %tile.3) | copy-start | bytes 4718596
where the time goes:
time: 68.8 us; the launch traced here: 68.7 us
  Pallas kernels  67.3 us (98%)
  local copies, waits for them, and re-layouts  1.41 us (2%)
    pallas_call x1, Pallas kernels, call_window(): pl.pallas_call(window, out_shape=jax.ShapeDtypeStruct((1, fields, height,...  57.9 us
    pallas_call x1, Pallas kernels, call_exchange(): pl.pallas_call(exchange, out_shape=(shape((2, fields, 8, width)), shape((...  9.4 us
    unnamed x4, local copies, waits for them, and re-layouts  1.41 us

commit v1 on v0

--- a/solution.py
+++ b/solution.py
@@ -137,14 +137,15 @@
     return e, u, v, h * u, h * v
 
 
-def change(above, here, below):
+def change(above, here, below, slopes):
     e0, u0, v0, hu0, _ = above
     e, u, v, _, hv = here
     e1, u1, v1, hu1, _ = below
+    along_e, along_u, along_v = slopes
     return (
         (hu1 - hu0) + along_cols(hv),
-        u * (u1 - u0) + v * (along_cols(u) - TURN) + (e1 - e0),
-        u * ((v1 - v0) + TURN) + v * along_cols(v) + along_cols(e),
+        u * (u1 - u0) + v * (along_u - TURN) + (e1 - e0),
+        u * ((v1 - v0) + TURN) + v * along_v + along_e,
     )
 
 
@@ -173,50 +174,105 @@
     return tuple(a - 0.5 * b for a, b in zip(state, rate))
 
 
-def sweep(ref, use):
+def band():
+    source = lax.broadcasted_iota(jnp.int32, (2 * LANES, LANES), 0) % LANES
+    target = lax.broadcasted_iota(jnp.int32, (2 * LANES, LANES), 1)
+    ahead = jnp.where(source == target + 1, 1.0, 0.0)
+    return (ahead - jnp.where(source == target - 1, 1.0, 0.0)).astype(jnp.bfloat16)
+
+
+def put_slopes(matrix, places):
+    values = jnp.concatenate([x for _, _, state in places for x in state], axis=0)
+    main = values.astype(jnp.bfloat16)
+    rest = (values - main.astype(jnp.float32)).astype(jnp.bfloat16)
+    out = jnp.dot(
+        jnp.concatenate([main, rest], axis=1), matrix[...], preferred_element_type=jnp.float32
+    )
+    for i, (ref, k, _) in enumerate(places):
+        for f in range(3):
+            at = (3 * i + f) * SUBS
+            ref[f, k] = out[at : at + SUBS]
+
+
+CHUNK = 5
+
+
+def chunk_ends(count):
+    return [min(k + CHUNK, count) for k in range(0, count, CHUNK)]
+
+
+def sweep(ref, slope, use):
     count = ref.shape[1]
     above = full(from_above(row_of(ref, count - 1)))
     here = first = full(row_of(ref, 0))
     last = full(from_below(first[:3]))
     for k in range(count):
         below = last if k == count - 1 else full(row_of(ref, k + 1))
-        use(k, here[:3], change(above, here, below))
+        use(k, here[:3], change(above, here, below, row_of(slope, k)))
         above, here = here, below
 
 
-def predict(pred):
-    sweep(pred, lambda k, state, rate: put_row(pred, k, minus(state, rate)))
-
-
-def first_step(pred, base):
+def stepping(pred, pred_slope, matrix, each):
+    ends = chunk_ends(pred.shape[1])
+    places = []
+
     def use(k, state, rate):
-        put_row(pred, k, minus(state, rate))
+        after = minus(state, rate)
+        put_row(pred, k, after)
+        places.append((pred_slope, k, after))
+        places.extend(each(k, state, rate))
+        if k + 1 in ends:
+            put_slopes(matrix, places)
+            places.clear()
+
+    sweep(pred, pred_slope, use)
+
+
+def predict(pred, pred_slope, matrix):
+    stepping(pred, pred_slope, matrix, lambda k, state, rate: [])
+
+
+def first_step(pred, pred_slope, matrix, base):
+    def each(k, state, rate):
         put_row(base, k, minus_half(state, rate))
-
-    sweep(pred, use)
-
-
-def middle_step(pred, base):
+        return []
+
+    stepping(pred, pred_slope, matrix, each)
+
+
+def middle_step(pred, pred_slope, matrix, base, corr, corr_slope):
     count = pred.shape[1]
-    corr = {}
-
-    def correct(k, above, here, below):
-        put_row(base, k, minus(row_of(base, k), change(above, here, below)))
-
-    def use(k, state, rate):
-        put_row(pred, k, minus(state, rate))
-        corr[k] = full(minus_half(row_of(base, k), rate))
-        if k >= 2:
-            correct(k - 1, corr[k - 2], corr[k - 1], corr[k])
-
-    sweep(pred, use)
-    end = count - 1
-    correct(end, corr[end - 1], corr[end], full(from_below(corr[0][:3])))
-    correct(0, full(from_above(corr[end][:3])), corr[0], corr[1])
-
-
-def last_step(pred, base):
-    sweep(pred, lambda k, state, rate: put_row(pred, k, minus_half(row_of(base, k), rate)))
+    held = {}
+
+    def correct(upto):
+        if "next" not in held:
+            held["next"], held["above"], held["here"] = 1, full(row_of(corr, 0)), full(row_of(corr, 1))
+        while held["next"] < upto:
+            k = held["next"]
+            if k == count - 1:
+                below = full(from_below(row_of(corr, 0)))
+            else:
+                below = full(row_of(corr, k + 1))
+            rate = change(held["above"], held["here"], below, row_of(corr_slope, k))
+            put_row(base, k, minus(row_of(base, k), rate))
+            held["next"], held["above"], held["here"] = k + 1, held["here"], below
+
+    def each(k, state, rate):
+        value = minus_half(row_of(base, k), rate)
+        put_row(corr, k, value)
+        if k >= 2 * CHUNK:
+            correct(k - 2 * CHUNK + 2)
+        return [(corr_slope, k, value)]
+
+    stepping(pred, pred_slope, matrix, each)
+    correct(count)
+    above = full(from_above(row_of(corr, count - 1)))
+    rate = change(above, full(row_of(corr, 0)), full(row_of(corr, 1)), row_of(corr_slope, 0))
+    put_row(base, 0, minus(row_of(base, 0), rate))
+
+
+def last_step(pred, pred_slope, base):
+    sweep(pred, pred_slope, lambda k, state, rate: put_row(pred, k, minus_half(row_of(base, k), rate)))
 
 
 def strip_plan(width):
@@ -229,7 +285,8 @@
 
 
 def window(
-    tile, rows, nine, cols, diag, out, padded, result, pred, base, load_sem, halo_sem, out_sem
+    tile, rows, nine, cols, diag, out, padded, result, pred, base, corr, pred_slope, corr_slope, matrix,
+    load_sem, halo_sem, out_sem
 ):
     fields, height, width = tile.shape
     tiles = width // LANES
@@ -275,6 +332,7 @@
     for load in loads:
         load.wait()
 
+    matrix[...] = band()
     lane = lax.broadcasted_iota(jnp.int32, (SUBS, LANES), 1)
     into = (ELEV, VEL, VEL)
 
@@ -290,21 +348,31 @@
         a = start // LANES
         offset = start - a * LANES
         from_first = lane >= offset
-        for f in range(fields):
-            for k in range(count):
-                at = pl.ds(TOP - DEPTH + k, SUBS, stride=count)
+        places = []
+        for k in range(count):
+            at = pl.ds(TOP - DEPTH + k, SUBS, stride=count)
+            state = ()
+            for f in range(fields):
                 both = jnp.where(from_first, padded[f, a, at, :], padded[f, a + 1, at, :])
-                pred[f, k] = into[f] * pltpu.roll(both, LANES - offset, 1)
+                state += (into[f] * pltpu.roll(both, LANES - offset, 1),)
+            put_row(pred, k, state)
+            places.append((pred_slope, k, state))
+        put_slopes(matrix, places)
 
         @pl.when(level == 0)
         def _():
-            lax.fori_loop(0, STEPS, lambda m, x: (predict(pred), x)[1], 0)
+            lax.fori_loop(0, STEPS, lambda m, x: (predict(pred, pred_slope, matrix), x)[1], 0)
 
         @pl.when(level == 1)
         def _():
-            first_step(pred, base)
-            lax.fori_loop(1, STEPS, lambda m, x: (middle_step(pred, base), x)[1], 0)
-            last_step(pred, base)
+            first_step(pred, pred_slope, matrix, base)
+
+            def middle(m, x):
+                middle_step(pred, pred_slope, matrix, base, corr, corr_slope)
+                return x
+
+            lax.fori_loop(1, STEPS, middle, 0)
+            last_step(pred, pred_slope, base)
 
         source = jnp.where(from_first, lane - offset, lane - offset + LANES)
         inside = (source >= DEPTH) & (source < DEPTH + stride)
@@ -347,6 +415,10 @@
             vmem(fields, tiles + 2, padded_rows, LANES),
             vmem(fields, count, SUBS, LANES),
             vmem(fields, count, SUBS, LANES),
+            vmem(fields, count, SUBS, LANES),
+            vmem(fields, count, SUBS, LANES),
+            vmem(fields, count, SUBS, LANES),
+            pltpu.VMEM((2 * LANES, LANES), jnp.bfloat16),
             pltpu.SemaphoreType.DMA((tiles,)),
             pltpu.SemaphoreType.DMA((2, tiles)),
             pltpu.SemaphoreType.DMA((tiles,)),

time: 68.8 us -> 45.2 us (0.66)
  Pallas kernels: 67.3 us -> 43.6 us
    pallas_call x1, Pallas kernels: 57.9 us -> 34.2 us  [call_window(): pl.pallas_call(window, out_shape=jax.ShapeDtypeStruct((1, fields, height,...]
where the time goes in v1:
time: 45.2 us; the launch traced here: 45 us
  Pallas kernels  43.6 us (96%)
  local copies, waits for them, and re-layouts  1.41 us (3%)
    pallas_call x1, Pallas kernels, call_window(): pl.pallas_call(window, out_shape=jax.ShapeDtypeStruct((1, fields, height,...  34.2 us
    pallas_call x1, Pallas kernels, call_exchange(): pl.pallas_call(exchange, out_shape=(shape((2, fields, 8, width)), shape((...  9.4 us
    unnamed x4, local copies, waits for them, and re-layouts  1.41 us

profile of v1, /device:TPU:7, one launch (start us, length us, event | category | flops | bytes accessed | tf_op | source)
XLA Modules:
  0.0 45.0 jit_solution(7916542895066968959)
XLA Ops:
  0.0 0.0 copy-start
  0.0 1.4 %copy-done = f32[3,128,1024]{2,1,0:T(8,128)S(1)} copy-done((f32[3,128,1024]{2,1,0:T(8,128)S(1)}, f32[3,128,1024]{2,1,0:T(8,128)}, u32[]{:S(2)}) %copy-start) | copy-done | bytes 1572888
  1.4 0.0 copy-start.1
  1.4 9.4 %exchange.1 = (f32[2,3,8,1024]{3,2,1,0:T(8,128)S(1)}, f32[2,24,128]{2,1,0:T(8,128)S(1)}, f32[2,2,3,8,128]{4,3,2,1,0:T(8,128)S(1)}, f32[4,3,8,128]{3,2,1,0:T(8,128)S(1)}) custom-call(f32[3,128,1024]{2,1,0:T(8,128)S(1)} %copy-done), custom_call_target="tpu_custom_call" | custom-call | tf_op jit(solution)/shard_map/exchange/pallas_call | solution.py:103
  10.8 0.0 copy-done.1
  10.8 34.2 %window.1 = f32[1,3,128,1024]{3,2,1,0:T(8,128)} custom-call(f32[3,128,1024]{2,1,0:T(8,128)S(1)} %copy-done.1, f32[2,3,8,1024]{3,2,1,0:T(8,128)S(1)} %get-tuple-element.9.rows, f32[2,24,128]{2,1,0:T(8,128)S(1)} %get-tuple-element.10.nine, f32[2,2,3,8,128]{4,3,2,1,0:T(8,128)S(1)} %get-tuple-element.11.cols, f32[4,3,8,128]{3,2,1,0:T(8,128)S(1)} %get-tuple-element.12.diag), custom_call_target="tpu_custom_call" | custom-call | tf_op jit(solution)/shard_map/window/pallas_call | solution.py:408
Async XLA Ops:
  0.0 1.4 %copy-start = (f32[3,128,1024]{2,1,0:T(8,128)S(1)}, f32[3,128,1024]{2,1,0:T(8,128)}, u32[]{:S(2)}) copy-start(f32[3,128,1024]{2,1,0:T(8,128)} %tile.3) | copy-start | bytes 4718596
  1.4 9.4 %copy-start.1 = (f32[3,128,1024]{2,1,0:T(8,128)S(1)}, f32[3,128,1024]{2,1,0:T(8,128)}, u32[]{:S(2)}) copy-start(f32[3,128,1024]{2,1,0:T(8,128)} %tile.3) | copy-start | bytes 4718596

commit v2 on v1

--- a/solution.py
+++ b/solution.py
@@ -121,7 +121,7 @@
             pltpu.SemaphoreType.DMA((10,)),
         ],
         compiler_params=pltpu.CompilerParams(
-            collective_id=0, has_side_effects=True, vmem_limit_bytes=8 * 1024 * 1024
+            collective_id=0, has_side_effects=True, vmem_limit_bytes=65994752
         ),
         name="exchange",
     )(initial)
@@ -194,7 +194,7 @@
             ref[f, k] = out[at : at + SUBS]
 
 
-CHUNK = 5
+CHUNK = 19
 
 
 def chunk_ends(count):
@@ -329,8 +329,16 @@
         for j in range(tiles):
             padded[f, j + 1, pl.ds(TOP - DEPTH, 1), :] = nine[0, pl.ds(f * tiles + j, 1), :]
             padded[f, j + 1, pl.ds(TOP + height + DEPTH - 1, 1), :] = nine[1, pl.ds(f * tiles + j, 1), :]
-    for load in loads:
-        load.wait()
+    def await_tile(j):
+        pltpu.make_async_copy(
+            tile.at[:, :, pl.ds(0, LANES)], padded.at[:, j + 1, pl.ds(TOP, height), :], load_sem.at[j]
+        ).wait()
+        for side, at in ((0, TOP - 8), (1, TOP + height)):
+            pltpu.make_async_copy(
+                rows.at[side, :, :, pl.ds(0, LANES)],
+                padded.at[:, j + 1, pl.ds(at, 8), :],
+                halo_sem.at[side, j],
+            ).wait()
 
     matrix[...] = band()
     lane = lax.broadcasted_iota(jnp.int32, (SUBS, LANES), 1)
@@ -347,6 +355,11 @@
         start = t * stride + LANES - DEPTH
         a = start // LANES
         offset = start - a * LANES
+
+        @pl.when((a < tiles) & ((t == 0) | ((start - stride) // LANES < a)))
+        def _():
+            await_tile(a)
+
         from_first = lane >= offset
         places = []
         for k in range(count):
@@ -423,7 +436,7 @@
             pltpu.SemaphoreType.DMA((2, tiles)),
             pltpu.SemaphoreType.DMA((tiles,)),
         ],
-        compiler_params=pltpu.CompilerParams(vmem_limit_bytes=16 * 1024 * 1024),
+        compiler_params=pltpu.CompilerParams(vmem_limit_bytes=65994752),
         name="window",
     )(initial, rows, nine, cols, diag)
 

time: 45.2 us -> 44.4 us (0.982)
  local copies, waits for them, and re-layouts: 1.41 us -> 0 us
  Pallas kernels: 43.6 us -> 44.2 us
    unnamed x4 -> x0, local copies, waits for them, and re-layouts: 1.41 us -> none
    pallas_call x1, Pallas kernels: 34.2 us -> 35 us  [call_window(): pl.pallas_call(window, out_shape=jax.ShapeDtypeStruct((1, fields, height,...]
where the time goes in v2:
time: 44.4 us; the launch traced here: 44.2 us
  Pallas kernels  44.2 us (100%)
    pallas_call x1, Pallas kernels, call_window(): pl.pallas_call(window, out_shape=jax.ShapeDtypeStruct((1, fields, height,...  35 us
    pallas_call x1, Pallas kernels, call_exchange(): pl.pallas_call(exchange, out_shape=(shape((2, fields, 8, width)), shape((...  9.24 us

profile of v2, /device:TPU:7, one launch (start us, length us, event | category | flops | bytes accessed | tf_op | source)
XLA Modules:
  0.0 44.2 jit_solution(1939106953521133051)
XLA Ops:
  0.0 9.2 %exchange.1 = (f32[2,3,8,1024]{3,2,1,0:T(8,128)}, f32[2,24,128]{2,1,0:T(8,128)}, f32[2,2,3,8,128]{4,3,2,1,0:T(8,128)}, f32[4,3,8,128]{3,2,1,0:T(8,128)}) custom-call(f32[3,128,1024]{2,1,0:T(8,128)} %tile.3), custom_call_target="tpu_custom_call" | custom-call | tf_op jit(solution)/shard_map/exchange/pallas_call | solution.py:103
  9.2 35.0 %window.1 = f32[1,3,128,1024]{3,2,1,0:T(8,128)} custom-call(f32[3,128,1024]{2,1,0:T(8,128)} %tile.3, f32[2,3,8,1024]{3,2,1,0:T(8,128)} %get-tuple-element.9.rows, f32[2,24,128]{2,1,0:T(8,128)} %get-tuple-element.10.nine, f32[2,2,3,8,128]{4,3,2,1,0:T(8,128)} %get-tuple-element.11.cols, f32[4,3,8,128]{3,2,1,0:T(8,128)} %get-tuple-element.12.diag), custom_call_target="tpu_custom_call" | custom-call | tf_op jit(solution)/shard_map/window/pallas_call | solution.py:421
